TPU v7x, 32 devices: a whole 2x2x4 slice. The times are simulated.
32 devices in a mesh: site: 2 (over x), row: 4 (over z), col: 4 (over y, core).
Axes of the slice: x: 2, y: 2, z: 4, core: 2. Of those that a mesh axis runs over, the one named last changes fastest.
Arguments:
- pair_array: bfloat16 [128, 64, 128], P(('site', 'row'), 'col'), parts along dimension 0, may hold values from -6 to 6
- in_gain: float32 [128], replicated, may hold values from 0.25 to 1.75
- left_weight: bfloat16 [256, 128], P('site'), parts along dimension 0, may hold values from -0.5 to 0.5
- right_weight: bfloat16 [256, 128], P('site'), parts along dimension 0, may hold values from -0.5 to 0.5
- mid_gain: float32 [128], replicated, may hold values from 0.25 to 1.75
- out_weight: bfloat16 [256, 128], P('site'), parts along dimension 0, may hold values from -0.5 to 0.5
- out_gate: bfloat16 [256, 128], P('site'), parts along dimension 0, may hold values from -0.5 to 0.5
Outputs:
- triangle_out: bfloat16 [128, 64, 128], P(('site', 'row'), 'col'), parts along dimension 0
There are 2 independent parts, one for each index of `site`. A program takes and returns all parts, laid end to end along the dimension named above; an argument that names none is the same for every part. Nothing has to cross between parts.
All inputs are finite; a program needn't handle non-finite values.
Results may differ from a plain program's by a relative error of at most 0.012.
Values may be sent and summed in bfloat16 or wider, within the bound.
A program may use at most 64 MiB of HBM per device.

v0:
```python
import jax
import jax.numpy as jnp
from jax import lax
from jax.sharding import PartitionSpec as P


def norm_channels(values, channel_gain):
    centred = values - jnp.mean(values, axis=-1, keepdims=True)
    return (
        centred
        * lax.rsqrt(jnp.mean(centred * centred, axis=-1, keepdims=True) + 1e-05)
        * channel_gain
    )


def both_factors(pair_in, in_gain, left_weight, right_weight):
    ready = norm_channels(pair_in.astype(jnp.float32), in_gain).astype(jnp.bfloat16)
    ready = lax.optimization_barrier(ready)
    left = jnp.einsum("ijc,cd->ijd", ready, left_weight, preferred_element_type=jnp.float32)
    right = jnp.einsum("ijc,cd->ijd", ready, right_weight, preferred_element_type=jnp.float32)
    return (ready, left.astype(jnp.bfloat16), right.astype(jnp.bfloat16))


def finish_pair(mixed, ready, mid_gain, out_weight, out_gate):
    scaled = norm_channels(mixed.astype(jnp.float32), mid_gain).astype(jnp.bfloat16)
    scaled = lax.optimization_barrier(scaled)
    gate = jax.nn.sigmoid(
        jnp.einsum("ijc,cd->ijd", ready, out_gate, preferred_element_type=jnp.float32)
    )
    return (
        jnp.einsum("ijd,dc->ijc", scaled, out_weight, preferred_element_type=jnp.float32) * gate
    ).astype(jnp.bfloat16)


def body(pair_array, in_gain, left_weight, right_weight, mid_gain, out_weight, out_gate):
    ready, left, right = both_factors(pair_array, in_gain, left_weight, right_weight)
    count = pair_array.shape[0] * lax.axis_size("row")
    left_lines, right_lines = (
        lax.all_to_all(left, "row", split_axis=2, concat_axis=0, tiled=True),
        lax.all_to_all(right, "row", split_axis=2, concat_axis=0, tiled=True),
    )
    strip = jnp.einsum(
        "kid,kjd->ijd",
        lax.all_gather(left_lines, "col", axis=1, tiled=True),
        right_lines,
        preferred_element_type=jnp.float32,
    )
    strip = (strip * count ** (-0.5)).astype(jnp.bfloat16)
    mixed = lax.all_to_all(strip, "row", split_axis=0, concat_axis=2, tiled=True)
    return finish_pair(mixed, ready, mid_gain, out_weight, out_gate)


def solution(mesh):
    return jax.shard_map(
        body,
        mesh=mesh,
        in_specs=(
            P(("site", "row"), "col", None),
            P(),
            P("site", None),
            P("site", None),
            P(),
            P("site", None),
            P("site", None),
        ),
        out_specs=P(("site", "row"), "col", None),
        check_vma=False,
    )
```

profile of v0, /device:TPU:0, one launch (start us, length us, event | category | flops | bytes accessed | tf_op | source)
XLA Modules:
  0.0 46.4 jit_solution(6474242782185736790)
XLA Ops:
  0.0 0.0 copy-start
  0.0 0.0 copy-start.1
  0.0 1.0 %convert_reduce_fusion = f32[16,16]{1,0:T(8,128)S(1)} fusion(bf16[16,16,128]{2,1,0:T(8,128)(2,1)} %param.7), kind=kLoop, calls=%fused_computation.15 | loop fusion | flops 65280 | bytes 66560 | tf_op jit(solution)/shard_map/reduce_sum | solution.py:8
  1.0 0.0 copy-done.1
  1.0 0.2 fusion.10
  1.2 0.0 copy-start.4
  1.3 0.6 %copy-done.4 = f32[128]{0:T(128)S(1)} copy-done((f32[128]{0:T(128)S(1)}, f32[128]{0:T(128)}, u32[]{:S(2)}) %copy-start.4) | copy-done | bytes 536
  1.9 0.1 fusion.12
  2.0 0.0 copy-done
  2.0 0.1 convolution_convert_fusion.1
  2.2 0.4 copy.32
  2.6 1.2 %reshape.39 = bf16[4,2,4096]{2,1,0:T(2,128)(2,1)} reshape(bf16[128,16,16]{2,1,0:T(8,128)(2,1)S(1)} %bitcast.43) | data formatting | bytes 131072
  3.8 0.0 copy-start.2
  3.8 6.5 %all-to-all-start = ((bf16[4,2,4096]{2,1,0:T(2,128)(2,1)}), bf16[4,2,4096]{2,1,0:T(2,128)(2,1)S(1)}, u32[]{:S(2)}, u32[]{:S(2)}) async-start(bf16[4,2,4096]{2,1,0:T(2,128)(2,1)} %reshape.39), calls=%async_computation | async-start | bytes 131072 | tf_op jit(solution)/shard_map/all_to_all | solution.py:40
  10.3 0.0 copy-done.2
  10.3 0.1 convolution_convert_fusion
  10.4 0.4 copy.34
  10.9 1.2 %reshape.41 = bf16[4,2,4096]{2,1,0:T(2,128)(2,1)} reshape(bf16[128,16,16]{2,1,0:T(8,128)(2,1)S(1)} %bitcast.44) | data formatting | bytes 131072
  12.0 4.0 %all-to-all-done = bf16[4,2,4096]{2,1,0:T(2,128)(2,1)S(1)} async-done(((bf16[4,2,4096]{2,1,0:T(2,128)(2,1)}), bf16[4,2,4096]{2,1,0:T(2,128)(2,1)S(1)}, u32[]{:S(2)}, u32[]{:S(2)}) %all-to-all-start) | async-done | bytes 65568 | tf_op jit(solution)/shard_map/all_to_all | solution.py:40
  16.0 3.3 %all-to-all-start.1 = ((bf16[4,2,4096]{2,1,0:T(2,128)(2,1)}), bf16[4,2,4096]{2,1,0:T(2,128)(2,1)S(1)}, u32[]{:S(2)}, u32[]{:S(2)}) async-start(bf16[4,2,4096]{2,1,0:T(2,128)(2,1)} %reshape.41), calls=%async_computation.1 | async-start | bytes 131072 | tf_op jit(solution)/shard_map/all_to_all | solution.py:39
  19.3 0.4 reshape.40
  19.7 0.4 copy.33
  20.2 0.3 copy.37
  20.5 4.6 %all-to-all-done.1 = bf16[4,2,4096]{2,1,0:T(2,128)(2,1)S(1)} async-done(((bf16[4,2,4096]{2,1,0:T(2,128)(2,1)}), bf16[4,2,4096]{2,1,0:T(2,128)(2,1)S(1)}, u32[]{:S(2)}, u32[]{:S(2)}) %all-to-all-start.1) | async-done | bytes 65568 | tf_op jit(solution)/shard_map/all_to_all | solution.py:39
  25.0 0.4 reshape.42
  25.4 0.4 copy.35
  25.9 0.3 copy.36
  26.2 7.2 %all_gather.3 = bf16[64,64,32]{0,1,2:T(8,128)(2,1)S(1)} all-gather(bf16[64,16,32]{0,1,2:T(8,128)(2,1)S(1)} %copy.36), channel_id=1, replica_groups=mesh['site'=2,'row'=4,'col'=4] {'col'}, dimensions={1}, use_global_device_ids=true | all-gather | bytes 327680 | tf_op jit(solution)/shard_map/all_gather | solution.py:44
  33.4 0.4 fusion.1
  33.8 0.3 copy.38
  34.1 0.3 reshape.43
  34.4 8.1 %all_to_all.45 = bf16[4,2,4096]{2,1,0:T(2,128)(2,1)S(1)} all-to-all(bf16[4,2,4096]{2,1,0:T(2,128)(2,1)S(1)} %reshape.43), channel_id=1, replica_groups=mesh['site'=2,'row'=4,'col'=4] {'row'}, dimensions={0} | all-to-all | bytes 131072 | tf_op jit(solution)/shard_map/all_to_all | solution.py:49
  42.5 0.2 reshape.44
  42.7 0.1 fusion.7
  42.8 0.2 multiply_reduce_fusion
  43.1 0.3 copy.39
  43.4 0.0 copy-start.5
  43.5 0.3 reshape.32
  43.7 0.4 copy-done.5
  44.1 0.0 copy-start.3
  44.1 0.1 multiply_convert_fusion
  44.2 0.6 %copy-done.3 = bf16[128,128]{1,0:T(8,128)(2,1)S(1)} copy-done((bf16[128,128]{1,0:T(8,128)(2,1)S(1)}, bf16[128,128]{1,0:T(8,128)(2,1)}, u32[]{:S(2)}) %copy-start.3) | copy-done | bytes 32792
  44.9 0.0 copy-start.6
  44.9 0.1 fusion.14
  45.0 0.6 %copy-done.6 = bf16[128,128]{1,0:T(8,128)(2,1)S(1)} copy-done((bf16[128,128]{1,0:T(8,128)(2,1)S(1)}, bf16[128,128]{1,0:T(8,128)(2,1)}, u32[]{:S(2)}) %copy-start.6) | copy-done | bytes 32792
  45.6 0.8 %fusion.6 = bf16[16,16,128]{2,1,0:T(8,128)(2,1)} fusion(f32[16,16,128]{2,1,0:T(8,128)S(1)} %fusion.14, bf16[16,16,128]{2,1,0:T(8,128)(2,1)S(1)} %fusion.12, bf16[128,128]{1,0:T(8,128)(2,1)S(1)} %copy-done.6), kind=kOutput, calls=%fused_computation.8 | convolution fusion | flops 8552448 | bytes 294912 | tf_op jit(solution)/shard_map/ijc,cd->ijd/dot_general | solution.py:28
  (5 shorter events, 0.1 us)
Async XLA Ops:
  0.0 2.0 %copy-start = (bf16[128,128]{1,0:T(8,128)(2,1)S(1)}, bf16[128,128]{1,0:T(8,128)(2,1)}, u32[]{:S(2)}) copy-start(bf16[128,128]{1,0:T(8,128)(2,1)} %param.10) | copy-start | bytes 98308
  0.0 1.0 %copy-start.1 = (bf16[16,16,128]{2,1,0:T(8,128)(2,1)S(1)}, bf16[16,16,128]{2,1,0:T(8,128)(2,1)}, u32[]{:S(2)}) copy-start(bf16[16,16,128]{2,1,0:T(8,128)(2,1)} %param.7) | copy-start | bytes 196612
  1.2 0.7 %copy-start.4 = (f32[128]{0:T(128)S(1)}, f32[128]{0:T(128)}, u32[]{:S(2)}) copy-start(f32[128]{0:T(128)} %param.8) | copy-start | bytes 1540
  3.8 6.5 %copy-start.2 = (bf16[128,128]{1,0:T(8,128)(2,1)S(1)}, bf16[128,128]{1,0:T(8,128)(2,1)}, u32[]{:S(2)}) copy-start(bf16[128,128]{1,0:T(8,128)(2,1)} %param.9) | copy-start | bytes 98308
  3.8 12.2 %all-to-all-start = ((bf16[4,2,4096]{2,1,0:T(2,128)(2,1)}), bf16[4,2,4096]{2,1,0:T(2,128)(2,1)S(1)}, u32[]{:S(2)}, u32[]{:S(2)}) async-start(bf16[4,2,4096]{2,1,0:T(2,128)(2,1)} %reshape.39), calls=%async_computation | async-start | bytes 131072 | tf_op jit(solution)/shard_map/all_to_all | solution.py:40
  16.0 9.0 %all-to-all-start.1 = ((bf16[4,2,4096]{2,1,0:T(2,128)(2,1)}), bf16[4,2,4096]{2,1,0:T(2,128)(2,1)S(1)}, u32[]{:S(2)}, u32[]{:S(2)}) async-start(bf16[4,2,4096]{2,1,0:T(2,128)(2,1)} %reshape.41), calls=%async_computation.1 | async-start | bytes 131072 | tf_op jit(solution)/shard_map/all_to_all | solution.py:39
  43.4 0.7 %copy-start.5 = (f32[128]{0:T(128)S(1)}, f32[128]{0:T(128)}, u32[]{:S(2)}) copy-start(f32[128]{0:T(128)} %param.11) | copy-start | bytes 1540
  44.1 0.8 %copy-start.3 = (bf16[128,128]{1,0:T(8,128)(2,1)S(1)}, bf16[128,128]{1,0:T(8,128)(2,1)}, u32[]{:S(2)}) copy-start(bf16[128,128]{1,0:T(8,128)(2,1)} %param.12) | copy-start | bytes 98308
  44.9 0.8 %copy-start.6 = (bf16[128,128]{1,0:T(8,128)(2,1)S(1)}, bf16[128,128]{1,0:T(8,128)(2,1)}, u32[]{:S(2)}) copy-start(bf16[128,128]{1,0:T(8,128)(2,1)} %param.13) | copy-start | bytes 98308
where the time goes:
time: 47 us; the launch traced here: 46.4 us
  blocking collectives  15.3 us (33%)
  starting transfers between devices  9.76 us (21%)
  local copies, waits for them, and re-layouts  9.11 us (19%)
  waiting for transfers between devices  8.55 us (18%)
  other arithmetic  1.87 us (4%)
  matrix products  1.61 us (3%)
    all_to_all x1, blocking collectives, body(): lax.all_to_all(strip, 'row', split_axis=0, concat_axis=2, tiled=True)  8.11 us
    all_gather x1, blocking collectives, body(): lax.all_gather(left_lines, 'col', axis=1, tiled=True)  7.2 us
    all_to_all x1, starting transfers between devices, body(): lax.all_to_all(right, 'row', split_axis=2, concat_axis=0, tiled=True)  6.48 us
    unnamed x20, local copies, waits for them, and re-layouts  5.82 us
    all_to_all x1, waiting for transfers between devices, body(): lax.all_to_all(left, 'row', split_axis=2, concat_axis=0, tiled=True)  4.56 us
    all_to_all x1, waiting for transfers between devices, body(): lax.all_to_all(right, 'row', split_axis=2, concat_axis=0, tiled=True)  3.99 us
    all_to_all x1, starting transfers between devices, body(): lax.all_to_all(left, 'row', split_axis=2, concat_axis=0, tiled=True)  3.28 us
    reduce_sum x2, other arithmetic, norm_channels(): centred = values - jnp.mean(values, axis=-1, keepdims=True)  1.14 us
  transfers between devices with their start and end apart: 2, of which 2 were waited for; matrix products, arithmetic and copies ran while one was open for 6% of the time, Pallas kernels for 0%

commit v1 on v0

--- a/solution.py
+++ b/solution.py
@@ -1,6 +1,10 @@
+import functools
+
 import jax
 import jax.numpy as jnp
 from jax import lax
+from jax.experimental import pallas as pl
+from jax.experimental.pallas import tpu as pltpu
 from jax.sharding import PartitionSpec as P
 
 
@@ -50,9 +54,222 @@
     return finish_pair(mixed, ready, mid_gain, out_weight, out_gate)
 
 
+MESH = pl.DeviceIdType.MESH
+
+
+def flip(index, mask, count):
+    flipped, bit = 0, 1
+    while bit < count:
+        digit = (index // bit) % 2
+        flipped = flipped + bit * ((1 - digit) if mask & bit else digit)
+        bit *= 2
+    return flipped
+
+
+def fused(
+    count, halves, scale,
+    pair_hbm, in_gain_hbm, left_hbm, right_hbm, mid_gain_hbm, out_hbm, gate_hbm,
+    result,
+    pair, in_gain, left_w, right_w, mid_gain, out_w, gate_w,
+    ready, left_send, left_got, right, wide, part_send, part_got, own, gate,
+    load_sem, lsend_sem, lgot_sem, psend_sem, pgot_sem,
+):
+    row, col = lax.axis_index("row"), lax.axis_index("col")
+    lines, width = pair.shape[0], pair.shape[1]
+    piece = width // halves
+    barrier = pltpu.get_barrier_semaphore()
+    for mask in range(1, count):
+        pl.semaphore_signal(
+            barrier, inc=1, device_id={"col": flip(col, mask, count)}, device_id_type=MESH
+        )
+        pl.semaphore_signal(
+            barrier, inc=1, device_id={"row": flip(row, mask, count)}, device_id_type=MESH
+        )
+    loads = [
+        pltpu.make_async_copy(src, dst, load_sem.at[n])
+        for n, (src, dst) in enumerate(
+            [
+                (pair_hbm, pair), (in_gain_hbm, in_gain), (left_hbm, left_w),
+                (right_hbm, right_w), (mid_gain_hbm, mid_gain), (out_hbm, out_w),
+                (gate_hbm, gate_w),
+            ]
+        )
+    ]
+    for load in loads:
+        load.start()
+    loads[0].wait()
+    loads[1].wait()
+    channels = pair.shape[2]
+    values = pair[...].reshape(lines * width, channels).astype(jnp.float32)
+    ready[...] = norm_channels(values, in_gain[...]).astype(jnp.bfloat16)
+    loads[2].wait()
+    left = jnp.dot(ready[...], left_w[...], preferred_element_type=jnp.float32)
+    depth = left.shape[-1]
+    left = left.reshape(lines, halves, piece, depth)
+    for half in range(halves):
+        left_send[half] = left[:, half].reshape(lines * piece, depth).astype(jnp.bfloat16)
+    loads[3].wait()
+    right[...] = (
+        jnp.dot(ready[...], right_w[...], preferred_element_type=jnp.float32)
+        .astype(jnp.bfloat16).astype(jnp.float32)
+    )
+
+    pl.semaphore_wait(barrier, 2 * (count - 1))
+
+    def left_copy(mask, half):
+        return pltpu.make_async_remote_copy(
+            src_ref=left_send.at[half],
+            dst_ref=left_got.at[mask - 1, half],
+            send_sem=lsend_sem.at[mask - 1, half],
+            recv_sem=lgot_sem.at[mask - 1, half],
+            device_id={"col": flip(col, mask, count)},
+            device_id_type=MESH,
+        )
+
+    for half in range(halves):
+        for mask in range(1, count):
+            left_copy(mask, half).start()
+
+    def part_copy(mask, half):
+        return pltpu.make_async_remote_copy(
+            src_ref=part_send.at[mask, half],
+            dst_ref=part_got.at[row, half],
+            send_sem=psend_sem.at[mask, half],
+            recv_sem=pgot_sem.at[row, half],
+            device_id={"row": flip(col, mask, count)},
+            device_id_type=MESH,
+        )
+
+    def products(mask, half):
+        source = left_send.at[half] if mask == 0 else left_got.at[mask - 1, half]
+        wide[...] = source[...].astype(jnp.float32)
+
+        def total():
+            sums = [None] * piece
+            for k in range(lines):
+                across = right[k * width : (k + 1) * width, :]
+                for i in range(piece):
+                    at = k * piece + i
+                    term = wide[at : at + 1, :] * across
+                    sums[i] = term if k == 0 else sums[i] + term
+            return sums
+
+        target = flip(col, mask, count)
+        sums = total()
+
+        @pl.when(target == row)
+        def _():
+            for i in range(piece):
+                own[half, i * width : (i + 1) * width, :] = sums[i]
+
+        @pl.when(target != row)
+        def _():
+            for i in range(piece):
+                part_send[mask, half, i * width : (i + 1) * width, :] = sums[i].astype(jnp.bfloat16)
+            part_copy(mask, half).start()
+
+    for mask in range(count):
+        for half in range(halves):
+            if mask >= 2:
+                break
+            if mask:
+                left_copy(mask, half).wait_recv()
+            products(mask, half)
+    loads[6].wait()
+    gate[...] = jax.nn.sigmoid(
+        jnp.dot(ready[...], gate_w[...], preferred_element_type=jnp.float32)
+    )
+    for half in range(halves):
+        for mask in range(2, count):
+            left_copy(mask, half).wait_recv()
+            products(mask, half)
+    loads[4].wait()
+    loads[5].wait()
+    for half in range(halves):
+        mixed = own[half]
+        for mask in range(1, count):
+            peer = flip(row, mask, count)
+            pltpu.make_async_remote_copy(
+                src_ref=part_send.at[0, half],
+                dst_ref=part_got.at[peer, half],
+                send_sem=psend_sem.at[0, half],
+                recv_sem=pgot_sem.at[peer, half],
+                device_id={"row": peer},
+                device_id_type=MESH,
+            ).wait_recv()
+            mixed = mixed + part_got[peer, half].astype(jnp.float32)
+        mixed = (mixed * scale).astype(jnp.bfloat16).astype(jnp.float32)
+        scaled = norm_channels(mixed, mid_gain[...]).astype(jnp.bfloat16)
+        rows = piece * width
+        made = jnp.dot(scaled, out_w[...], preferred_element_type=jnp.float32)
+        made = made * gate[half * rows : (half + 1) * rows, :]
+        result[half * piece : (half + 1) * piece] = made.astype(jnp.bfloat16).reshape(
+            piece, width, channels
+        )
+    for half in range(halves):
+        for mask in range(1, count):
+            left_copy(mask, half).wait_send()
+        for mask in range(count):
+
+            @pl.when(flip(col, mask, count) != row)
+            def _(mask=mask, half=half):
+                part_copy(mask, half).wait_send()
+
+
+def fused_body(pair_array, in_gain, left_weight, right_weight, mid_gain, out_weight, out_gate):
+    count = lax.axis_size("row")
+    lines, width, channels = pair_array.shape
+    depth = left_weight.shape[1]
+    halves = max(width // 8, 1)
+    piece = width // halves
+    scale = (lines * count) ** (-0.5)
+    low, high = jnp.bfloat16, jnp.float32
+    return pl.pallas_call(
+        functools.partial(fused, count, halves, scale),
+        out_shape=jax.ShapeDtypeStruct(pair_array.shape, low),
+        in_specs=[pl.BlockSpec(memory_space=pl.ANY)] * 7,
+        out_specs=pl.BlockSpec(memory_space=pltpu.VMEM),
+        scratch_shapes=[
+            pltpu.VMEM(pair_array.shape, low),
+            pltpu.VMEM((1, channels), high),
+            pltpu.VMEM(left_weight.shape, low),
+            pltpu.VMEM(right_weight.shape, low),
+            pltpu.VMEM((1, depth), high),
+            pltpu.VMEM(out_weight.shape, low),
+            pltpu.VMEM(out_gate.shape, low),
+            pltpu.VMEM((lines * width, channels), low),
+            pltpu.VMEM((halves, lines * piece, depth), low),
+            pltpu.VMEM((count - 1, halves, lines * piece, depth), low),
+            pltpu.VMEM((lines * width, depth), high),
+            pltpu.VMEM((lines * piece, depth), high),
+            pltpu.VMEM((count, halves, piece * width, depth), low),
+            pltpu.VMEM((count, halves, piece * width, depth), low),
+            pltpu.VMEM((halves, piece * width, depth), high),
+            pltpu.VMEM((lines * width, channels), high),
+            pltpu.SemaphoreType.DMA((7,)),
+            pltpu.SemaphoreType.DMA((count - 1, halves)),
+            pltpu.SemaphoreType.DMA((count - 1, halves)),
+            pltpu.SemaphoreType.DMA((count, halves)),
+            pltpu.SemaphoreType.DMA((count, halves)),
+        ],
+        compiler_params=pltpu.CompilerParams(collective_id=0, has_side_effects=True),
+        name="triangle",
+    )(
+        pair_array, in_gain.reshape(1, -1), left_weight, right_weight,
+        mid_gain.reshape(1, -1), out_weight, out_gate,
+    )
+
+
+def pick(pair_array, *rest):
+    rows, cols = lax.axis_size("row"), lax.axis_size("col")
+    square = rows == cols and rows & (rows - 1) == 0
+    square = square and pair_array.shape[0] == pair_array.shape[1]
+    return (fused_body if square else body)(pair_array, *rest)
+
+
 def solution(mesh):
     return jax.shard_map(
-        body,
+        pick,
         mesh=mesh,
         in_specs=(
             P(("site", "row"), "col", None),

time: 47 us -> 16.2 us (0.34)
  the two profiles are of different devices: /device:TPU:0 before, /device:TPU:5 now
where the time goes in v1:
time: 16.2 us; the launch traced here: 16 us
  Pallas kernels  14.5 us (90%)
  local copies, waits for them, and re-layouts  1.47 us (9%)
    pallas_call x1, Pallas kernels, fused_body(): pl.pallas_call(functools.partial(fused, count, halves, scale), out_shape=...  14.5 us
    unnamed x1, local copies, waits for them, and re-layouts  1.47 us

profile of v1, /device:TPU:5, one launch (start us, length us, event | category | flops | bytes accessed | tf_op | source)
XLA Modules:
  0.0 16.0 jit_solution(214435863070706233)
XLA Ops:
  0.0 14.5 %triangle.1 = bf16[16,16,128]{2,1,0:T(8,128)(2,1)} custom-call(bf16[16,16,128]{2,1,0:T(8,128)(2,1)} %pair_hbm.1, f32[1,128]{1,0:T(1,128)} %bitcast.2, bf16[128,128]{1,0:T(8,128)(2,1)} %left_hbm.1, bf16[128,128]{1,0:T(8,128)(2,1)} %right_hbm.1, f32[1,128]{1,0:T(1,128)} %bitcast.3, bf16[128,128]{1,0:T(8,128)(2,1)} %out_hbm.1, bf16[128,128]{1,0:T(8,128)(2,1)} %gate_hbm.1), custom_call_target="tpu_custom_call" | custom-call | tf_op jit(solution)/shard_map/triangle/pallas_call | solution.py:227
  14.5 1.5 %copy.9 = bf16[16,16,128]{2,1,0:T(8,128)(2,1)} copy(bf16[16,16,128]{2,1,0:T(8,128)(2,1)} %triangle.1) | data formatting | bytes 131072

commit v2 on v0

--- a/solution.py
+++ b/solution.py
@@ -1,6 +1,10 @@
+import functools
+
 import jax
 import jax.numpy as jnp
 from jax import lax
+from jax.experimental import pallas as pl
+from jax.experimental.pallas import tpu as pltpu
 from jax.sharding import PartitionSpec as P
 
 
@@ -50,9 +54,235 @@
     return finish_pair(mixed, ready, mid_gain, out_weight, out_gate)
 
 
+MESH = pl.DeviceIdType.MESH
+
+
+def flip(index, mask, count):
+    flipped, bit = 0, 1
+    while bit < count:
+        digit = (index // bit) % 2
+        flipped = flipped + bit * ((1 - digit) if mask & bit else digit)
+        bit *= 2
+    return flipped
+
+
+def fused(
+    count, scale,
+    pair_hbm, in_gain_hbm, left_hbm, right_hbm, mid_gain_hbm, out_hbm, gate_hbm,
+    result,
+    pair, in_gain, left_w, right_w, mid_gain, out_w, gate_w,
+    ready, left_send, left_got, right_send, right_got, right, wide, part_send, part_got, own, gate,
+    load_sem, lsend_sem, lgot_sem, rsend_sem, rgot_sem, psend_sem, pgot_sem,
+):
+    row, col = lax.axis_index("row"), lax.axis_index("col")
+    half = col % 2
+    twin = flip(col, 1, count)
+    lines, width = pair.shape[0], pair.shape[1]
+    piece = width // 2
+    barrier = pltpu.get_barrier_semaphore()
+    for mask in range(1, count):
+        there = flip(row, mask, count)
+        for device in ({"col": flip(col, mask, count)}, {"row": there}, {"row": there, "col": twin}):
+            pl.semaphore_signal(barrier, inc=1, device_id=device, device_id_type=MESH)
+    loads = [
+        pltpu.make_async_copy(src, dst, load_sem.at[n])
+        for n, (src, dst) in enumerate(
+            [
+                (pair_hbm, pair), (in_gain_hbm, in_gain), (left_hbm, left_w),
+                (right_hbm, right_w), (mid_gain_hbm, mid_gain), (out_hbm, out_w),
+                (gate_hbm, gate_w),
+            ]
+        )
+    ]
+    for load in loads:
+        load.start()
+    loads[0].wait()
+    loads[1].wait()
+    channels = pair.shape[2]
+    values = pair[...].reshape(lines * width, channels).astype(jnp.float32)
+    ready[...] = norm_channels(values, in_gain[...]).astype(jnp.bfloat16)
+    loads[2].wait()
+    left = jnp.dot(ready[...], left_w[...], preferred_element_type=jnp.float32)
+    depth = left.shape[-1]
+    left = left.reshape(lines, 2, piece, depth)
+    for part in range(2):
+        left_send[part] = left[:, part].reshape(lines * piece, depth).astype(jnp.bfloat16)
+    loads[3].wait()
+    right_send[...] = jnp.dot(
+        ready[...], right_w[...], preferred_element_type=jnp.float32
+    ).astype(jnp.bfloat16)
+
+    pl.semaphore_wait(barrier, 3 * (count - 1))
+
+    def left_copy(mask):
+        return pltpu.make_async_remote_copy(
+            src_ref=left_send.at[(half + mask) % 2],
+            dst_ref=left_got.at[mask - 1],
+            send_sem=lsend_sem.at[mask - 1],
+            recv_sem=lgot_sem.at[mask - 1],
+            device_id={"col": flip(col, mask, count)},
+            device_id_type=MESH,
+        )
+
+    right_copy = pltpu.make_async_remote_copy(
+        src_ref=right_send,
+        dst_ref=right_got,
+        send_sem=rsend_sem,
+        recv_sem=rgot_sem,
+        device_id={"col": twin},
+        device_id_type=MESH,
+    )
+    for mask in range(2, count):
+        left_copy(mask).start()
+    right_copy.start()
+    left_copy(1).start()
+
+    def part_copy(mask, side):
+        return pltpu.make_async_remote_copy(
+            src_ref=part_send.at[mask, side],
+            dst_ref=part_got.at[row, half],
+            send_sem=psend_sem.at[mask, side],
+            recv_sem=pgot_sem.at[row, half],
+            device_id={"row": flip(col, mask, count), "col": twin if side else col},
+            device_id_type=MESH,
+        )
+
+    def products(mask, side):
+        sums = [None] * piece
+        for k in range(lines):
+            across = right[side, k * width : (k + 1) * width, :]
+            for i in range(piece):
+                at = k * piece + i
+                term = wide[mask, at : at + 1, :] * across
+                sums[i] = term if k == 0 else sums[i] + term
+
+        def send():
+            for i in range(piece):
+                part_send[mask, side, i * width : (i + 1) * width, :] = sums[i].astype(jnp.bfloat16)
+            part_copy(mask, side).start()
+
+        if side:
+            send()
+        else:
+            here = flip(col, mask, count) == row
+
+            @pl.when(here)
+            def _():
+                for i in range(piece):
+                    own[i * width : (i + 1) * width, :] = sums[i]
+
+            pl.when(jnp.logical_not(here))(send)
+
+    right[0] = right_send[...].astype(jnp.float32)
+    wide[0] = left_send[half].astype(jnp.float32)
+    products(0, 0)
+    right_copy.wait_recv()
+    right[1] = right_got[...].astype(jnp.float32)
+    products(0, 1)
+    for mask in range(1, count):
+        left_copy(mask).wait_recv()
+        wide[mask] = left_got[mask - 1].astype(jnp.float32)
+        products(mask, 0)
+        products(mask, 1)
+        if mask == 1:
+            loads[6].wait()
+            gate[...] = jax.nn.sigmoid(
+                jnp.dot(ready[...], gate_w[...], preferred_element_type=jnp.float32)
+            )
+    loads[4].wait()
+    loads[5].wait()
+
+    def arrived(peer, part):
+        pltpu.make_async_remote_copy(
+            src_ref=part_send.at[0, 0],
+            dst_ref=part_got.at[peer, part],
+            send_sem=psend_sem.at[0, 0],
+            recv_sem=pgot_sem.at[peer, part],
+            device_id={"row": row, "col": twin},
+            device_id_type=MESH,
+        ).wait_recv()
+        return part_got[peer, part].astype(jnp.float32)
+
+    rows = piece * width
+    for part, mixed in ((half, own[...]), (1 - half, arrived(row, 1 - half))):
+        for mask in range(1, count):
+            mixed = mixed + arrived(flip(row, mask, count), part)
+        mixed = (mixed * scale).astype(jnp.bfloat16).astype(jnp.float32)
+        scaled = norm_channels(mixed, mid_gain[...]).astype(jnp.bfloat16)
+        made = jnp.dot(scaled, out_w[...], preferred_element_type=jnp.float32)
+        made = made * gate[pl.ds(pl.multiple_of(part * rows, rows), rows), :]
+        result[pl.ds(part * piece, piece)] = made.astype(jnp.bfloat16).reshape(
+            piece, width, channels
+        )
+    for mask in range(1, count):
+        left_copy(mask).wait_send()
+    right_copy.wait_send()
+    for mask in range(count):
+        part_copy(mask, 1).wait_send()
+
+        @pl.when(flip(col, mask, count) != row)
+        def _(mask=mask):
+            part_copy(mask, 0).wait_send()
+
+
+def fused_body(pair_array, in_gain, left_weight, right_weight, mid_gain, out_weight, out_gate):
+    count = lax.axis_size("row")
+    lines, width, channels = pair_array.shape
+    depth = left_weight.shape[1]
+    piece = width // 2
+    scale = (lines * count) ** (-0.5)
+    low, high = jnp.bfloat16, jnp.float32
+    return pl.pallas_call(
+        functools.partial(fused, count, scale),
+        out_shape=jax.ShapeDtypeStruct(pair_array.shape, low),
+        in_specs=[pl.BlockSpec(memory_space=pl.ANY)] * 7,
+        out_specs=pl.BlockSpec(memory_space=pltpu.VMEM),
+        scratch_shapes=[
+            pltpu.VMEM(pair_array.shape, low),
+            pltpu.VMEM((1, channels), high),
+            pltpu.VMEM(left_weight.shape, low),
+            pltpu.VMEM(right_weight.shape, low),
+            pltpu.VMEM((1, depth), high),
+            pltpu.VMEM(out_weight.shape, low),
+            pltpu.VMEM(out_gate.shape, low),
+            pltpu.VMEM((lines * width, channels), low),
+            pltpu.VMEM((2, lines * piece, depth), low),
+            pltpu.VMEM((count - 1, lines * piece, depth), low),
+            pltpu.VMEM((lines * width, depth), low),
+            pltpu.VMEM((lines * width, depth), low),
+            pltpu.VMEM((2, lines * width, depth), high),
+            pltpu.VMEM((count, lines * piece, depth), high),
+            pltpu.VMEM((count, 2, piece * width, depth), low),
+            pltpu.VMEM((count, 2, piece * width, depth), low),
+            pltpu.VMEM((piece * width, depth), high),
+            pltpu.VMEM((lines * width, channels), high),
+            pltpu.SemaphoreType.DMA((7,)),
+            pltpu.SemaphoreType.DMA((count - 1,)),
+            pltpu.SemaphoreType.DMA((count - 1,)),
+            pltpu.SemaphoreType.DMA,
+            pltpu.SemaphoreType.DMA,
+            pltpu.SemaphoreType.DMA((count, 2)),
+            pltpu.SemaphoreType.DMA((count, 2)),
+        ],
+        compiler_params=pltpu.CompilerParams(collective_id=0, has_side_effects=True),
+        name="triangle",
+    )(
+        pair_array, in_gain.reshape(1, -1), left_weight, right_weight,
+        mid_gain.reshape(1, -1), out_weight, out_gate,
+    )
+
+
+def pick(pair_array, *rest):
+    rows, cols = lax.axis_size("row"), lax.axis_size("col")
+    square = rows == cols > 1 and rows & (rows - 1) == 0
+    square = square and pair_array.shape[0] == pair_array.shape[1]
+    square = square and pair_array.shape[1] % 16 == 0
+    return (fused_body if square else body)(pair_array, *rest)
+
+
 def solution(mesh):
     return jax.shard_map(
-        body,
+        pick,
         mesh=mesh,
         in_specs=(
             P(("site", "row"), "col", None),

time: 47 us -> 15.5 us (0.33)
  the two profiles are of different devices: /device:TPU:0 before, /device:TPU:25 now
where the time goes in v2:
time: 15.5 us; the launch traced here: 15.3 us
  Pallas kernels  13.8 us (89%)
  local copies, waits for them, and re-layouts  1.47 us (9%)
    pallas_call x1, Pallas kernels, fused_body(): pl.pallas_call(functools.partial(fused, count, scale), out_shape=jax.Shap...  13.8 us
    unnamed x1, local copies, waits for them, and re-layouts  1.47 us

profile of v2, /device:TPU:25, one launch (start us, length us, event | category | flops | bytes accessed | tf_op | source)
XLA Modules:
  0.0 15.3 jit_solution(16011292219220635417)
XLA Ops:
  0.0 13.8 %triangle.1 = bf16[16,16,128]{2,1,0:T(8,128)(2,1)} custom-call(bf16[16,16,128]{2,1,0:T(8,128)(2,1)} %pair_hbm.1, f32[1,128]{1,0:T(1,128)} %bitcast.2, bf16[128,128]{1,0:T(8,128)(2,1)} %left_hbm.1, bf16[128,128]{1,0:T(8,128)(2,1)} %right_hbm.1, f32[1,128]{1,0:T(1,128)} %bitcast.3, bf16[128,128]{1,0:T(8,128)(2,1)} %out_hbm.1, bf16[128,128]{1,0:T(8,128)(2,1)} %gate_hbm.1), custom_call_target="tpu_custom_call" | custom-call | tf_op jit(solution)/shard_map/triangle/pallas_call | solution.py:235
  13.8 1.5 %copy.9 = bf16[16,16,128]{2,1,0:T(8,128)(2,1)} copy(bf16[16,16,128]{2,1,0:T(8,128)(2,1)} %triangle.1) | data formatting | bytes 131072

commit v3 on v2

--- a/solution.py
+++ b/solution.py
@@ -234,7 +234,7 @@
     low, high = jnp.bfloat16, jnp.float32
     return pl.pallas_call(
         functools.partial(fused, count, scale),
-        out_shape=jax.ShapeDtypeStruct(pair_array.shape, low),
+        out_shape=pltpu.VMEM(pair_array.shape, low),
         in_specs=[pl.BlockSpec(memory_space=pl.ANY)] * 7,
         out_specs=pl.BlockSpec(memory_space=pltpu.VMEM),
         scratch_shapes=[

time: 15.5 us -> 14 us (0.903)
  local copies, waits for them, and re-layouts: 1.47 us -> 0.63 us
  Pallas kernels: 13.8 us -> 13.2 us
    unnamed x1, local copies, waits for them, and re-layouts: 1.47 us -> 0.63 us
    pallas_call x1, Pallas kernels: 13.8 us -> 13.2 us  [fused_body(): pl.pallas_call(functools.partial(fused, count, scale), out_shape=pltpu.VM...]
where the time goes in v3:
time: 14 us; the launch traced here: 13.9 us
  Pallas kernels  13.2 us (94%)
  local copies, waits for them, and re-layouts  0.63 us (4%)
    pallas_call x1, Pallas kernels, fused_body(): pl.pallas_call(functools.partial(fused, count, scale), out_shape=pltpu.VM...  13.2 us
    unnamed x1, local copies, waits for them, and re-layouts  0.63 us

profile of v3, /device:TPU:25, one launch (start us, length us, event | category | flops | bytes accessed | tf_op | source)
XLA Modules:
  0.0 13.9 jit_solution(17466480336747566878)
XLA Ops:
  0.0 13.2 %triangle.1 = bf16[16,16,128]{2,1,0:T(8,128)(2,1)S(1)} custom-call(bf16[16,16,128]{2,1,0:T(8,128)(2,1)} %pair_hbm.1, f32[1,128]{1,0:T(1,128)} %bitcast.2, bf16[128,128]{1,0:T(8,128)(2,1)} %left_hbm.1, bf16[128,128]{1,0:T(8,128)(2,1)} %right_hbm.1, f32[1,128]{1,0:T(1,128)} %bitcast.3, bf16[128,128]{1,0:T(8,128)(2,1)} %out_hbm.1, bf16[128,128]{1,0:T(8,128)(2,1)} %gate_hbm.1), custom_call_target="tpu_custom_call" | custom-call | tf_op jit(solution)/shard_map/triangle/pallas_call | solution.py:235
  13.2 0.6 %copy.9 = bf16[16,16,128]{2,1,0:T(8,128)(2,1)} copy(bf16[16,16,128]{2,1,0:T(8,128)(2,1)S(1)} %triangle.1) | data formatting | bytes 131072

commit v4 on v3

--- a/solution.py
+++ b/solution.py
@@ -73,6 +73,7 @@
     pair, in_gain, left_w, right_w, mid_gain, out_w, gate_w,
     ready, left_send, left_got, right_send, right_got, right, wide, part_send, part_got, own, gate,
     load_sem, lsend_sem, lgot_sem, rsend_sem, rgot_sem, psend_sem, pgot_sem,
+    near_sem, far_sem,
 ):
     row, col = lax.axis_index("row"), lax.axis_index("col")
     half = col % 2
@@ -80,10 +81,18 @@
     lines, width = pair.shape[0], pair.shape[1]
     piece = width // 2
     barrier = pltpu.get_barrier_semaphore()
+    for n in range(count // 2):
+        odd = 2 * n + 1
+
+        @pl.when(odd != col)
+        def _(odd=odd):
+            pl.semaphore_signal(barrier, inc=1, device_id={"col": odd}, device_id_type=MESH)
+
     for mask in range(1, count):
-        there = flip(row, mask, count)
-        for device in ({"col": flip(col, mask, count)}, {"row": there}, {"row": there, "col": twin}):
-            pl.semaphore_signal(barrier, inc=1, device_id=device, device_id_type=MESH)
+        pl.semaphore_signal(
+            barrier, inc=1, device_id={"row": flip(row, mask, count), "col": col - half},
+            device_id_type=MESH,
+        )
     loads = [
         pltpu.make_async_copy(src, dst, load_sem.at[n])
         for n, (src, dst) in enumerate(
@@ -112,7 +121,14 @@
         ready[...], right_w[...], preferred_element_type=jnp.float32
     ).astype(jnp.bfloat16)
 
-    pl.semaphore_wait(barrier, 3 * (count - 1))
+    @pl.when(half == 1)
+    def _():
+        pl.semaphore_wait(barrier, count - 1)
+        pl.semaphore_signal(near_sem, inc=1, device_id={"col": twin}, device_id_type=MESH)
+
+    @pl.when(half == 0)
+    def _():
+        pl.semaphore_wait(near_sem, 1)
 
     def left_copy(mask):
         return pltpu.make_async_remote_copy(
@@ -175,6 +191,20 @@
 
     right[0] = right_send[...].astype(jnp.float32)
     wide[0] = left_send[half].astype(jnp.float32)
+    loads[6].wait()
+    gate[...] = jax.nn.sigmoid(
+        jnp.dot(ready[...], gate_w[...], preferred_element_type=jnp.float32)
+    )
+
+    @pl.when(half == 0)
+    def _():
+        pl.semaphore_wait(barrier, 2 * (count - 1))
+        pl.semaphore_signal(far_sem, inc=1, device_id={"col": twin}, device_id_type=MESH)
+
+    @pl.when(half == 1)
+    def _():
+        pl.semaphore_wait(far_sem, 1)
+
     products(0, 0)
     right_copy.wait_recv()
     right[1] = right_got[...].astype(jnp.float32)
@@ -184,11 +214,6 @@
         wide[mask] = left_got[mask - 1].astype(jnp.float32)
         products(mask, 0)
         products(mask, 1)
-        if mask == 1:
-            loads[6].wait()
-            gate[...] = jax.nn.sigmoid(
-                jnp.dot(ready[...], gate_w[...], preferred_element_type=jnp.float32)
-            )
     loads[4].wait()
     loads[5].wait()
 
@@ -263,6 +288,8 @@
             pltpu.SemaphoreType.DMA,
             pltpu.SemaphoreType.DMA((count, 2)),
             pltpu.SemaphoreType.DMA((count, 2)),
+            pltpu.SemaphoreType.REGULAR,
+            pltpu.SemaphoreType.REGULAR,
         ],
         compiler_params=pltpu.CompilerParams(collective_id=0, has_side_effects=True),
         name="triangle",

time: 14 us -> 14.2 us (1.014)
  the two profiles are of different devices: /device:TPU:25 before, /device:TPU:0 now
where the time goes in v4:
time: 14.2 us; the launch traced here: 14 us
  Pallas kernels  13.4 us (94%)
  local copies, waits for them, and re-layouts  0.63 us (4%)
    pallas_call x1, Pallas kernels, fused_body(): pl.pallas_call(functools.partial(fused, count, scale), out_shape=pltpu.VM...  13.4 us
    unnamed x1, local copies, waits for them, and re-layouts  0.63 us

profile of v4, /device:TPU:0, one launch (start us, length us, event | category | flops | bytes accessed | tf_op | source)
XLA Modules:
  0.0 14.0 jit_solution(6297013091037749831)
XLA Ops:
  0.0 13.4 %triangle.1 = bf16[16,16,128]{2,1,0:T(8,128)(2,1)S(1)} custom-call(bf16[16,16,128]{2,1,0:T(8,128)(2,1)} %pair_hbm.1, f32[1,128]{1,0:T(1,128)} %bitcast.2, bf16[128,128]{1,0:T(8,128)(2,1)} %left_hbm.1, bf16[128,128]{1,0:T(8,128)(2,1)} %right_hbm.1, f32[1,128]{1,0:T(1,128)} %bitcast.3, bf16[128,128]{1,0:T(8,128)(2,1)} %out_hbm.1, bf16[128,128]{1,0:T(8,128)(2,1)} %gate_hbm.1), custom_call_target="tpu_custom_call" | custom-call | tf_op jit(solution)/shard_map/triangle/pallas_call | solution.py:260
  13.4 0.6 %copy.9 = bf16[16,16,128]{2,1,0:T(8,128)(2,1)} copy(bf16[16,16,128]{2,1,0:T(8,128)(2,1)S(1)} %triangle.1) | data formatting | bytes 131072

commit v5 on v4

--- a/solution.py
+++ b/solution.py
@@ -172,13 +172,12 @@
                 term = wide[mask, at : at + 1, :] * across
                 sums[i] = term if k == 0 else sums[i] + term
 
-        def send():
+        def keep():
             for i in range(piece):
                 part_send[mask, side, i * width : (i + 1) * width, :] = sums[i].astype(jnp.bfloat16)
-            part_copy(mask, side).start()
 
         if side:
-            send()
+            keep()
         else:
             here = flip(col, mask, count) == row
 
@@ -187,7 +186,16 @@
                 for i in range(piece):
                     own[i * width : (i + 1) * width, :] = sums[i]
 
-            pl.when(jnp.logical_not(here))(send)
+            pl.when(jnp.logical_not(here))(keep)
+
+    def launch(mask, side):
+        if side:
+            part_copy(mask, side).start()
+        else:
+
+            @pl.when(flip(col, mask, count) != row)
+            def _():
+                part_copy(mask, side).start()
 
     right[0] = right_send[...].astype(jnp.float32)
     wide[0] = left_send[half].astype(jnp.float32)
@@ -195,15 +203,6 @@
     gate[...] = jax.nn.sigmoid(
         jnp.dot(ready[...], gate_w[...], preferred_element_type=jnp.float32)
     )
-
-    @pl.when(half == 0)
-    def _():
-        pl.semaphore_wait(barrier, 2 * (count - 1))
-        pl.semaphore_signal(far_sem, inc=1, device_id={"col": twin}, device_id_type=MESH)
-
-    @pl.when(half == 1)
-    def _():
-        pl.semaphore_wait(far_sem, 1)
 
     products(0, 0)
     right_copy.wait_recv()
@@ -213,7 +212,23 @@
         left_copy(mask).wait_recv()
         wide[mask] = left_got[mask - 1].astype(jnp.float32)
         products(mask, 0)
+        if mask > 1:
+            launch(mask, 0)
         products(mask, 1)
+        if mask > 1:
+            launch(mask, 1)
+        else:
+            @pl.when(half == 0)
+            def _():
+                pl.semaphore_wait(barrier, 2 * (count - 1))
+                pl.semaphore_signal(far_sem, inc=1, device_id={"col": twin}, device_id_type=MESH)
+
+            @pl.when(half == 1)
+            def _():
+                pl.semaphore_wait(far_sem, 1)
+            for early in range(2):
+                for side in range(2):
+                    launch(early, side)
     loads[4].wait()
     loads[5].wait()
 

time: 14.2 us -> 14.9 us (1.049)
  Pallas kernels: 13.4 us -> 14.1 us
    pallas_call x1, Pallas kernels: 13.4 us -> 14.1 us  [fused_body(): pl.pallas_call(functools.partial(fused, count, scale), out_shape=pltpu.VM...]
where the time goes in v5:
time: 14.9 us; the launch traced here: 14.7 us
  Pallas kernels  14.1 us (95%)
  local copies, waits for them, and re-layouts  0.63 us (4%)
    pallas_call x1, Pallas kernels, fused_body(): pl.pallas_call(functools.partial(fused, count, scale), out_shape=pltpu.VM...  14.1 us
    unnamed x1, local copies, waits for them, and re-layouts  0.63 us

profile of v5, /device:TPU:0, one launch (start us, length us, event | category | flops | bytes accessed | tf_op | source)
XLA Modules:
  0.0 14.7 jit_solution(14421709842230981300)
XLA Ops:
  0.0 14.1 %triangle.1 = bf16[16,16,128]{2,1,0:T(8,128)(2,1)S(1)} custom-call(bf16[16,16,128]{2,1,0:T(8,128)(2,1)} %pair_hbm.1, f32[1,128]{1,0:T(1,128)} %bitcast.2, bf16[128,128]{1,0:T(8,128)(2,1)} %left_hbm.1, bf16[128,128]{1,0:T(8,128)(2,1)} %right_hbm.1, f32[1,128]{1,0:T(1,128)} %bitcast.3, bf16[128,128]{1,0:T(8,128)(2,1)} %out_hbm.1, bf16[128,128]{1,0:T(8,128)(2,1)} %gate_hbm.1), custom_call_target="tpu_custom_call" | custom-call | tf_op jit(solution)/shard_map/triangle/pallas_call | solution.py:275
  14.1 0.6 %copy.9 = bf16[16,16,128]{2,1,0:T(8,128)(2,1)} copy(bf16[16,16,128]{2,1,0:T(8,128)(2,1)S(1)} %triangle.1) | data formatting | bytes 131072
